TPU v7x, 32 devices: a whole 2x2x4 slice. The times are simulated.
32 devices in a mesh: kpt: 4 (over y, x), pw: 8 (over z, core).
Axes of the slice: x: 2, y: 2, z: 4, core: 2. Of those that a mesh axis runs over, the one named last changes fastest.
Arguments:
- energies: float32 [16, 512], P('kpt', 'pw'), may hold values from 0.5 to 3
- current: float32 [2, 16, 512], P(None, 'kpt', 'pw'), may hold values from -40 to 40
- previous: float32 [2, 16, 512], P(None, 'kpt', 'pw'), may hold values from -6 to 6
- previous_beta: float32 [2], replicated, may hold values from 0.5 to 2
- pair_left: bfloat16 [16, 512, 4096], P('kpt', None, 'pw'), may hold values from -0.09375 to 0.09375
- pair_right: bfloat16 [16, 512, 4096], P('kpt', None, 'pw'), may hold values from -0.25 to 0.25
- screened: bfloat16 [16, 4096, 4096], P('kpt', 'pw'), may hold values from -0.0234375 to 0.0234375
- momentum_index: int32 [16, 16], replicated, may hold values from 0 to 15, each once within a row
Outputs:
- last_vector: float32 [2, 16, 512], P(None, 'kpt', 'pw')
- prior_vector: float32 [2, 16, 512], P(None, 'kpt', 'pw')
- alpha_terms: float32 [2, 3], replicated
- beta_terms: float32 [2, 3], replicated
Inputs may be any that keep to these rules, and one draw needn't show every extreme that they name: Each row of momentum_index names every index from 0 to 15 once.
All inputs are finite; a program needn't handle non-finite values.
Results may differ from a plain program's by a relative error of at most 0.003.
Values may be sent and summed in bfloat16 or wider, within the bound.
A program may use at most 128 MiB of HBM per device.

v0:
```python
import jax
import jax.numpy as jnp
from jax import lax
from jax.sharding import PartitionSpec as P

STEPS = 3
epsilon = 1e-06


def screened_images(density, screened):
    kpoint_rows = lax.all_gather(density, "kpt", axis=0, tiled=True)
    return jnp.einsum(
        "qsg,kvg->qkvs",
        screened,
        lax.all_gather(kpoint_rows, "pw", axis=2, tiled=True),
        preferred_element_type=jnp.float32,
    )


def on_device(
    energies, current, previous, previous_beta, pair_left, pair_right, screened, momentum_index
):
    kpoint_total = momentum_index.shape[0]
    band_total = pair_left.shape[1]
    entries = kpoint_total * band_total
    qcount = screened.shape[0]
    qpoints = lax.axis_index("kpt") * qcount + jnp.arange(qcount, dtype=jnp.int32)
    selector = (momentum_index[None, :, :] == qpoints[:, None, None]).astype(jnp.float32)
    vector, earlier, levels = (current, previous, energies)
    beta_before = previous_beta
    alpha_list = []
    beta_list = []
    for turn_index in range(STEPS):
        rounded = vector.astype(jnp.bfloat16)
        rounded = lax.all_gather(rounded, "pw", axis=2, tiled=True)
        density = jnp.einsum(
            "kcg,vkc->kvg", pair_right, rounded, preferred_element_type=jnp.float32
        ).astype(jnp.bfloat16)
        images = screened_images(density, screened)
        partial_field = jnp.einsum(
            "qjk,qkvs->jvs",
            selector,
            images,
            precision=lax.Precision.HIGHEST,
            preferred_element_type=jnp.float32,
        )
        potential = lax.psum_scatter(partial_field, "kpt", scatter_dimension=0, tiled=True).astype(
            jnp.bfloat16
        )
        partial_direct = jnp.einsum(
            "kcs,kvs->vkc", pair_left, potential, preferred_element_type=jnp.float32
        )
        direct = lax.psum_scatter(partial_direct, "pw", scatter_dimension=2, tiled=True)
        applied = levels[None] * vector - direct - beta_before[:, None, None] * earlier
        vector_own = vector
        cross_sum, square_sum, vector_sum = lax.psum(
            (
                jnp.sum(vector_own * applied, axis=(1, 2)),
                jnp.sum(applied * applied, axis=(1, 2)),
                jnp.sum(vector_own * vector_own, axis=(1, 2)),
            ),
            ("kpt", "pw"),
        )
        alpha_now = cross_sum / entries
        mean_square = (
            square_sum / entries
            - 2.0 * alpha_now * (cross_sum / entries)
            + alpha_now * alpha_now * (vector_sum / entries)
        )
        beta_now = jnp.sqrt(mean_square + epsilon)
        residual = applied - alpha_now[:, None, None] * vector
        earlier = vector
        vector = residual / beta_now[:, None, None]
        beta_before = beta_now
        alpha_list.append(alpha_now)
        beta_list.append(beta_now)
    return (vector, earlier, jnp.stack(alpha_list, axis=1), jnp.stack(beta_list, axis=1))


def solution(mesh):
    return jax.shard_map(
        on_device,
        mesh=mesh,
        in_specs=(
            P("kpt", "pw"),
            P(None, "kpt", "pw"),
            P(None, "kpt", "pw"),
            P(),
            P("kpt", None, "pw"),
            P("kpt", None, "pw"),
            P("kpt", "pw", None),
            P(),
        ),
        out_specs=(P(None, "kpt", "pw"), P(None, "kpt", "pw"), P(), P()),
        check_vma=False,
    )
```

profile of v0, /device:TPU:10, one launch (start us, length us, event | category | flops | bytes accessed | tf_op | source)
XLA Modules:
  0.0 434.7 jit_solution(2461469843560152316)
XLA Ops:
  8.2 14.4 %all_gather.27 = bf16[2,4,512]{1,0,2:T(2,128)(2,1)S(1)} all-gather(bf16[2,4,64]{1,0,2:T(2,128)(2,1)S(1)} %copy.33), channel_id=1, replica_groups=mesh['kpt'=4,'pw'=8] {'pw'}, dimensions={2}, use_global_device_ids=true | all-gather | bytes 9216 | tf_op jit(solution)/shard_map/all_gather | solution.py:35
  23.2 8.2 %all_gather.28 = bf16[16,2,512]{2,1,0:T(2,128)(2,1)S(1)} all-gather(bf16[4,2,512]{2,1,0:T(2,128)(2,1)S(1)} %convolution_convert_fusion.2), channel_id=1, replica_groups=mesh['kpt'=4,'pw'=8] {'kpt'}, dimensions={0}, use_global_device_ids=true | all-gather | bytes 40960 | tf_op jit(solution)/shard_map/all_gather | solution.py:11
  31.4 14.3 %all_gather.29 = bf16[16,2,4096]{2,0,1:T(8,128)(2,1)S(1)} all-gather(bf16[16,2,512]{2,0,1:T(8,128)(2,1)S(1)} %copy.35), channel_id=1, replica_groups=mesh['kpt'=4,'pw'=8] {'pw'}, dimensions={2}, use_global_device_ids=true | all-gather | bytes 294912 | tf_op jit(solution)/shard_map/all_gather | solution.py:15
  45.6 10.8 %fusion.6 = f32[4,16,2,512]{3,1,0,2:T(8,128)S(1)} fusion(bf16[4,512,4096]{2,1,0:T(8,128)(2,1)} %param.14, bf16[16,2,4096]{2,0,1:T(8,128)(2,1)S(1)} %all_gather.29), kind=kOutput, calls=%fused_computation.6 | convolution fusion | flops 536870912 | bytes 17301504 | tf_op jit(solution)/shard_map/qsg,kvg->qkvs/dot_general | solution.py:12
  56.9 15.0 %all-reduce = bf16[16,2,512]{2,1,0:T(2,128)(2,1)S(1)} all-reduce(f32[16,2,512]{2,1,0:T(2,128)S(1)} %copy.36), channel_id=2, replica_groups=mesh['kpt'=4,'pw'=8] {'kpt'}, use_global_device_ids=true, to_apply=%region_0.0.clone | all-reduce | flops 16384 | bytes 98304
  73.2 2.2 convolution_bitcast_fusion.5
  77.1 28.3 %reduce-scatter.10.cloned.1.call-done = f32[64,8]{1,0:T(8,128)} async-done(((f32[512,8]{1,0:T(8,128)}), f32[64,8]{1,0:T(8,128)}) %reduce-scatter.10.cloned.1.call-update) | async-done | bytes 2064
  106.6 43.5 %all-reduce.5 = (f32[2]{0:T(128)S(1)}, f32[2]{0:T(128)S(1)}, f32[2]{0:T(128)S(1)}) all-reduce(f32[2]{0:T(128)S(1)} %get-tuple-element.24, f32[2]{0:T(128)S(1)} %get-tuple-element.23, f32[2]{0:T(128)S(1)} %get-tuple-element.22), channel_id=1, replica_groups=mesh['kpt'=4,'pw'=8] {'kpt','pw'}, use_global_device_ids=true, to_apply=%region_7.0 | all-reduce | flops 6 | bytes 48 | tf_op jit(solution)/shard_map/psum | solution.py:56
  150.4 12.4 %all_gather.30 = bf16[2,4,512]{1,0,2:T(2,128)(2,1)S(1)} all-gather(bf16[2,4,64]{1,0,2:T(2,128)(2,1)S(1)} %copy.38), channel_id=1, replica_groups=mesh['kpt'=4,'pw'=8] {'pw'}, dimensions={2}, use_global_device_ids=true | all-gather | bytes 9216 | tf_op jit(solution)/shard_map/all_gather | solution.py:35
  163.3 7.2 %all_gather.31 = bf16[16,2,512]{2,1,0:T(2,128)(2,1)S(1)} all-gather(bf16[4,2,512]{2,1,0:T(2,128)(2,1)S(1)} %convolution_convert_fusion.1), channel_id=1, replica_groups=mesh['kpt'=4,'pw'=8] {'kpt'}, dimensions={0}, use_global_device_ids=true | all-gather | bytes 40960 | tf_op jit(solution)/shard_map/all_gather | solution.py:11
  170.5 14.4 %all_gather.32 = bf16[16,2,4096]{2,0,1:T(8,128)(2,1)S(1)} all-gather(bf16[16,2,512]{2,0,1:T(8,128)(2,1)S(1)} %copy.40), channel_id=1, replica_groups=mesh['kpt'=4,'pw'=8] {'pw'}, dimensions={2}, use_global_device_ids=true | all-gather | bytes 294912 | tf_op jit(solution)/shard_map/all_gather | solution.py:15
  184.9 10.8 %fusion.9 = f32[4,16,2,512]{3,1,0,2:T(8,128)S(1)} fusion(bf16[4,512,4096]{2,1,0:T(8,128)(2,1)} %param.14, bf16[16,2,4096]{2,0,1:T(8,128)(2,1)S(1)} %all_gather.32), kind=kOutput, calls=%fused_computation.7 | convolution fusion | flops 536870912 | bytes 17301504 | tf_op jit(solution)/shard_map/qsg,kvg->qkvs/dot_general | solution.py:12
  196.2 15.7 %all-reduce.1 = bf16[16,2,512]{2,1,0:T(2,128)(2,1)S(1)} all-reduce(f32[16,2,512]{2,1,0:T(2,128)S(1)} %copy.41), channel_id=4, replica_groups=mesh['kpt'=4,'pw'=8] {'kpt'}, use_global_device_ids=true, to_apply=%region_8.0.clone | all-reduce | flops 16384 | bytes 98304
  211.8 2.2 convolution_bitcast_fusion.4
  215.8 27.7 %reduce-scatter.12.cloned.1.call-done = f32[64,8]{1,0:T(8,128)} async-done(((f32[512,8]{1,0:T(8,128)}), f32[64,8]{1,0:T(8,128)}) %reduce-scatter.12.cloned.1.call-update) | async-done | bytes 2064
  244.7 43.5 %all-reduce.4 = (f32[2]{0:T(128)S(1)}, f32[2]{0:T(128)S(1)}, f32[2]{0:T(128)S(1)}) all-reduce(f32[2]{0:T(128)S(1)} %get-tuple-element.21, f32[2]{0:T(128)S(1)} %get-tuple-element.20, f32[2]{0:T(128)S(1)} %get-tuple-element.19), channel_id=1, replica_groups=mesh['kpt'=4,'pw'=8] {'kpt','pw'}, use_global_device_ids=true, to_apply=%region_15.0 | all-reduce | flops 6 | bytes 48 | tf_op jit(solution)/shard_map/psum | solution.py:56
  288.3 12.4 %all_gather.33 = bf16[2,4,512]{1,0,2:T(2,128)(2,1)S(1)} all-gather(bf16[2,4,64]{1,0,2:T(2,128)(2,1)S(1)} %copy.43), channel_id=1, replica_groups=mesh['kpt'=4,'pw'=8] {'pw'}, dimensions={2}, use_global_device_ids=true | all-gather | bytes 9216 | tf_op jit(solution)/shard_map/all_gather | solution.py:35
  301.3 7.3 %all_gather.34 = bf16[16,2,512]{2,1,0:T(2,128)(2,1)S(1)} all-gather(bf16[4,2,512]{2,1,0:T(2,128)(2,1)S(1)} %convolution_convert_fusion), channel_id=1, replica_groups=mesh['kpt'=4,'pw'=8] {'kpt'}, dimensions={0}, use_global_device_ids=true | all-gather | bytes 40960 | tf_op jit(solution)/shard_map/all_gather | solution.py:11
  308.6 14.2 %all_gather.35 = bf16[16,2,4096]{2,0,1:T(8,128)(2,1)S(1)} all-gather(bf16[16,2,512]{2,0,1:T(8,128)(2,1)S(1)} %copy.45), channel_id=1, replica_groups=mesh['kpt'=4,'pw'=8] {'pw'}, dimensions={2}, use_global_device_ids=true | all-gather | bytes 294912 | tf_op jit(solution)/shard_map/all_gather | solution.py:15
  322.8 10.8 %fusion.12 = f32[4,16,2,512]{3,1,0,2:T(8,128)S(1)} fusion(bf16[4,512,4096]{2,1,0:T(8,128)(2,1)} %param.14, bf16[16,2,4096]{2,0,1:T(8,128)(2,1)S(1)} %all_gather.35), kind=kOutput, calls=%fused_computation.8 | convolution fusion | flops 536870912 | bytes 17301504 | tf_op jit(solution)/shard_map/qsg,kvg->qkvs/dot_general | solution.py:12
  334.1 15.6 %all-reduce.2 = bf16[16,2,512]{2,1,0:T(2,128)(2,1)S(1)} all-reduce(f32[16,2,512]{2,1,0:T(2,128)S(1)} %copy.46), channel_id=6, replica_groups=mesh['kpt'=4,'pw'=8] {'kpt'}, use_global_device_ids=true, to_apply=%region_16.0.clone | all-reduce | flops 16384 | bytes 98304
  349.6 2.2 convolution_bitcast_fusion.3
  353.5 28.0 %reduce-scatter.14.cloned.1.call-done = f32[64,8]{1,0:T(8,128)} async-done(((f32[512,8]{1,0:T(8,128)}), f32[64,8]{1,0:T(8,128)}) %reduce-scatter.14.cloned.1.call-update) | async-done | bytes 2064
  382.7 43.5 %all-reduce.3 = (f32[2]{0:T(128)S(1)}, f32[2]{0:T(128)S(1)}, f32[2]{0:T(128)S(1)}) all-reduce(f32[2]{0:T(128)S(1)} %get-tuple-element.18, f32[2]{0:T(128)S(1)} %get-tuple-element.17, f32[2]{0:T(128)S(1)} %get-tuple-element.16), channel_id=1, replica_groups=mesh['kpt'=4,'pw'=8] {'kpt','pw'}, use_global_device_ids=true, to_apply=%region_23.0 | all-reduce | flops 6 | bytes 48 | tf_op jit(solution)/shard_map/psum | solution.py:56
  (68 shorter events, 15.3 us)
Async XLA Ops:
  7.2 15.6 %copy-start = (bf16[4,512,512]{2,1,0:T(8,128)(2,1)S(1)}, bf16[4,512,512]{2,1,0:T(8,128)(2,1)}, u32[]{:S(2)}) copy-start(bf16[4,512,512]{2,1,0:T(8,128)(2,1)} %param.13) | copy-start | bytes 6291460
  7.2 98.2 %reduce-scatter.10.cloned.1.call-start = ((), (), s32[]{:S(2)}) async-start(), calls=%async_computation.3 | async-start | bytes 294912
  45.6 10.8 %copy-start.1 = (s32[16,16]{1,0:T(8,128)S(1)}, s32[16,16]{1,0:T(8,128)}, u32[]{:S(2)}) copy-start(s32[16,16]{1,0:T(8,128)} %param.15) | copy-start | bytes 3076
  45.6 26.3 %copy-start.7 = (u32[32]{0:T(128)S(1)}, u32[32]{0:T(128)}, u32[]{:S(2)}) copy-start(u32[32]{0:T(128)} %constant.29) | copy-start | bytes 388
  73.2 33.2 %copy-start.2 = (f32[2,4,64]{2,1,0:T(4,128)S(1)}, f32[2,4,64]{2,1,0:T(4,128)}, u32[]{:S(2)}) copy-start(f32[2,4,64]{2,1,0:T(4,128)} %param.9) | copy-start | bytes 6148
  73.2 33.2 %copy-start.4 = (f32[4,64]{1,0:T(4,128)S(1)}, f32[4,64]{1,0:T(4,128)}, u32[]{:S(2)}) copy-start(f32[4,64]{1,0:T(4,128)} %param.8) | copy-start | bytes 3076
  73.2 33.2 %copy-start.5 = (f32[2,4,64]{2,1,0:T(4,128)S(1)}, f32[2,4,64]{2,1,0:T(4,128)}, u32[]{:S(2)}) copy-start(f32[2,4,64]{2,1,0:T(4,128)} %param.10) | copy-start | bytes 6148
  73.2 33.2 %copy-start.6 = (f32[2]{0:T(128)S(1)}, f32[2]{0:T(128)}, u32[]{:S(2)}) copy-start(f32[2]{0:T(128)} %param.11) | copy-start | bytes 28
  77.1 166.4 %reduce-scatter.12.cloned.1.call-start = ((), (), s32[]{:S(2)}) async-start(), calls=%async_computation.4 | async-start | bytes 294912
  215.7 165.8 %reduce-scatter.14.cloned.1.call-start = ((), (), s32[]{:S(2)}) async-start(), calls=%async_computation.5 | async-start | bytes 294912
  288.2 139.3 %copy-start.3 = (f32[2,4,64]{2,1,0:T(4,128)}, f32[2,4,64]{2,1,0:T(4,128)S(1)}, u32[]{:S(2)}) copy-start(f32[2,4,64]{2,1,0:T(4,128)S(1)} %get-tuple-element.36) | copy-start | bytes 6148
Sparse Core Ops, SparseCore 0:
  77.2 28.1 reduce-scatter.9
  215.8 27.6 reduce-scatter.11
  353.6 27.8 reduce-scatter.13
where the time goes:
time: 436 us; the launch traced here: 435 us
  blocking collectives  282 us (65%)
  waiting for transfers between devices  84.1 us (19%)
  matrix products  41.3 us (9%)
  between operations  14.7 us (3%)
  local copies, waits for them, and re-layouts  10.7 us (2%)
    psum x3, blocking collectives, on_device(): lax.psum((jnp.sum(vector_own * applied, axis=(1, 2)), jnp.sum(applied * a...  130 us
    unnamed x6, waiting for transfers between devices  84.1 us
    unnamed x3, blocking collectives  46.3 us
    all_gather x3, blocking collectives, screened_images(): lax.all_gather(kpoint_rows, 'pw', axis=2, tiled=True)  42.9 us
    all_gather x3, blocking collectives, on_device(): rounded = lax.all_gather(rounded, 'pw', axis=2, tiled=True)  39.2 us
    dot_general x3, matrix products, screened_images(): jnp.einsum('qsg,kvg->qkvs', screened, lax.all_gather(kpoint_rows, 'pw', a...  32.4 us
    all_gather x3, blocking collectives, screened_images(): kpoint_rows = lax.all_gather(density, 'kpt', axis=0, tiled=True)  22.8 us
    unnamed x28, local copies, waits for them, and re-layouts  9.34 us
  transfers between devices with their start and end apart: 3, of which 3 were waited for; matrix products, arithmetic and copies ran while one was open for 0% of the time, Pallas kernels for 0%

commit v1 on v0

--- a/solution.py
+++ b/solution.py
@@ -54,12 +54,15 @@
         applied = levels[None] * vector - direct - beta_before[:, None, None] * earlier
         vector_own = vector
         cross_sum, square_sum, vector_sum = lax.psum(
-            (
-                jnp.sum(vector_own * applied, axis=(1, 2)),
-                jnp.sum(applied * applied, axis=(1, 2)),
-                jnp.sum(vector_own * vector_own, axis=(1, 2)),
+            lax.psum(
+                (
+                    jnp.sum(vector_own * applied, axis=(1, 2)),
+                    jnp.sum(applied * applied, axis=(1, 2)),
+                    jnp.sum(vector_own * vector_own, axis=(1, 2)),
+                ),
+                "pw",
             ),
-            ("kpt", "pw"),
+            "kpt",
         )
         alpha_now = cross_sum / entries
         mean_square = (

time: 436 us -> 387 us (0.89); the launches traced: 435 us -> 379 us
  blocking collectives: 282 us -> 224 us
    psum x3, blocking collectives: 130 us -> 42 us  [on_device(): lax.psum((jnp.sum(vector_own * applied, axis=(1, 2)), jnp.sum(applied * a...]
    psum x0 -> x3, blocking collectives: none -> 24.1 us  [on_device(): lax.psum(lax.psum((jnp.sum(vector_own * applied, axis=(1, 2)), jnp.sum(ap...]
    all_gather x3, blocking collectives: 39.2 us -> 43.6 us  [on_device(): rounded = lax.all_gather(rounded, 'pw', axis=2, tiled=True)]
where the time goes in v1:
time: 387 us; the launch traced here: 379 us
  blocking collectives  224 us (58%)
  waiting for transfers between devices  86.3 us (22%)
  matrix products  41.3 us (11%)
  between operations  14.7 us (4%)
  local copies, waits for them, and re-layouts  10.7 us (3%)
    unnamed x6, waiting for transfers between devices  86.3 us
    unnamed x3, blocking collectives  45 us
    all_gather x3, blocking collectives, on_device(): rounded = lax.all_gather(rounded, 'pw', axis=2, tiled=True)  43.6 us
    all_gather x3, blocking collectives, screened_images(): lax.all_gather(kpoint_rows, 'pw', axis=2, tiled=True)  42.9 us
    psum x3, blocking collectives, on_device(): lax.psum((jnp.sum(vector_own * applied, axis=(1, 2)), jnp.sum(applied * a...  42 us
    dot_general x3, matrix products, screened_images(): jnp.einsum('qsg,kvg->qkvs', screened, lax.all_gather(kpoint_rows, 'pw', a...  32.4 us
    all_gather x3, blocking collectives, screened_images(): kpoint_rows = lax.all_gather(density, 'kpt', axis=0, tiled=True)  26.3 us
    psum x3, blocking collectives, on_device(): lax.psum(lax.psum((jnp.sum(vector_own * applied, axis=(1, 2)), jnp.sum(ap...  24.1 us
  transfers between devices with their start and end apart: 3, of which 3 were waited for; matrix products, arithmetic and copies ran while one was open for 0% of the time, Pallas kernels for 0%

profile of v1, /device:TPU:10, one launch (start us, length us, event | category | flops | bytes accessed | tf_op | source)
XLA Modules:
  0.0 379.3 jit_solution(11969798153382101777)
XLA Ops:
  8.2 14.4 %all_gather.27 = bf16[2,4,512]{1,0,2:T(2,128)(2,1)S(1)} all-gather(bf16[2,4,64]{1,0,2:T(2,128)(2,1)S(1)} %copy.33), channel_id=1, replica_groups=mesh['kpt'=4,'pw'=8] {'pw'}, dimensions={2}, use_global_device_ids=true | all-gather | bytes 9216 | tf_op jit(solution)/shard_map/all_gather | solution.py:35
  23.2 8.2 %all_gather.28 = bf16[16,2,512]{2,1,0:T(2,128)(2,1)S(1)} all-gather(bf16[4,2,512]{2,1,0:T(2,128)(2,1)S(1)} %convolution_convert_fusion.2), channel_id=1, replica_groups=mesh['kpt'=4,'pw'=8] {'kpt'}, dimensions={0}, use_global_device_ids=true | all-gather | bytes 40960 | tf_op jit(solution)/shard_map/all_gather | solution.py:11
  31.4 14.3 %all_gather.29 = bf16[16,2,4096]{2,0,1:T(8,128)(2,1)S(1)} all-gather(bf16[16,2,512]{2,0,1:T(8,128)(2,1)S(1)} %copy.35), channel_id=1, replica_groups=mesh['kpt'=4,'pw'=8] {'pw'}, dimensions={2}, use_global_device_ids=true | all-gather | bytes 294912 | tf_op jit(solution)/shard_map/all_gather | solution.py:15
  45.7 10.8 %fusion.6 = f32[4,16,2,512]{3,1,0,2:T(8,128)S(1)} fusion(bf16[4,512,4096]{2,1,0:T(8,128)(2,1)} %param.14, bf16[16,2,4096]{2,0,1:T(8,128)(2,1)S(1)} %all_gather.29), kind=kOutput, calls=%fused_computation.6 | convolution fusion | flops 536870912 | bytes 17301504 | tf_op jit(solution)/shard_map/qsg,kvg->qkvs/dot_general | solution.py:12
  56.9 15.0 %all-reduce = bf16[16,2,512]{2,1,0:T(2,128)(2,1)S(1)} all-reduce(f32[16,2,512]{2,1,0:T(2,128)S(1)} %copy.36), channel_id=2, replica_groups=mesh['kpt'=4,'pw'=8] {'kpt'}, use_global_device_ids=true, to_apply=%region_0.0.clone | all-reduce | flops 16384 | bytes 98304
  77.1 28.5 %reduce-scatter.10.cloned.1.call-done = f32[64,8]{1,0:T(8,128)} async-done(((f32[512,8]{1,0:T(8,128)}), f32[64,8]{1,0:T(8,128)}) %reduce-scatter.10.cloned.1.call-update) | async-done | bytes 2064
  106.8 14.0 %all-reduce.5 = (f32[2]{0:T(128)S(1)}, f32[2]{0:T(128)S(1)}, f32[2]{0:T(128)S(1)}) all-reduce(f32[2]{0:T(128)S(1)} %get-tuple-element.24, f32[2]{0:T(128)S(1)} %get-tuple-element.23, f32[2]{0:T(128)S(1)} %get-tuple-element.22), channel_id=1, replica_groups=mesh['kpt'=4,'pw'=8] {'pw'}, use_global_device_ids=true, to_apply=%region_9.0 | all-reduce | flops 6 | bytes 48 | tf_op jit(solution)/shard_map/psum | solution.py:57
  120.8 8.1 %all-reduce.8 = (f32[2]{0:T(128)S(1)}, f32[2]{0:T(128)S(1)}, f32[2]{0:T(128)S(1)}) all-reduce(f32[2]{0:T(128)S(1)} %get-tuple-element.31, f32[2]{0:T(128)S(1)} %get-tuple-element.32, f32[2]{0:T(128)S(1)} %get-tuple-element.33), channel_id=1, replica_groups=mesh['kpt'=4,'pw'=8] {'kpt'}, use_global_device_ids=true, to_apply=%region_10.0 | all-reduce | flops 6 | bytes 48 | tf_op jit(solution)/shard_map/psum | solution.py:56
  129.1 14.6 %all_gather.30 = bf16[2,4,512]{1,0,2:T(2,128)(2,1)S(1)} all-gather(bf16[2,4,64]{1,0,2:T(2,128)(2,1)S(1)} %copy.38), channel_id=1, replica_groups=mesh['kpt'=4,'pw'=8] {'pw'}, dimensions={2}, use_global_device_ids=true | all-gather | bytes 9216 | tf_op jit(solution)/shard_map/all_gather | solution.py:35
  144.3 9.0 %all_gather.31 = bf16[16,2,512]{2,1,0:T(2,128)(2,1)S(1)} all-gather(bf16[4,2,512]{2,1,0:T(2,128)(2,1)S(1)} %convolution_convert_fusion.1), channel_id=1, replica_groups=mesh['kpt'=4,'pw'=8] {'kpt'}, dimensions={0}, use_global_device_ids=true | all-gather | bytes 40960 | tf_op jit(solution)/shard_map/all_gather | solution.py:11
  153.3 14.4 %all_gather.32 = bf16[16,2,4096]{2,0,1:T(8,128)(2,1)S(1)} all-gather(bf16[16,2,512]{2,0,1:T(8,128)(2,1)S(1)} %copy.40), channel_id=1, replica_groups=mesh['kpt'=4,'pw'=8] {'pw'}, dimensions={2}, use_global_device_ids=true | all-gather | bytes 294912 | tf_op jit(solution)/shard_map/all_gather | solution.py:15
  167.7 10.8 %fusion.9 = f32[4,16,2,512]{3,1,0,2:T(8,128)S(1)} fusion(bf16[4,512,4096]{2,1,0:T(8,128)(2,1)} %param.14, bf16[16,2,4096]{2,0,1:T(8,128)(2,1)S(1)} %all_gather.32), kind=kOutput, calls=%fused_computation.7 | convolution fusion | flops 536870912 | bytes 17301504 | tf_op jit(solution)/shard_map/qsg,kvg->qkvs/dot_general | solution.py:12
  178.9 15.0 %all-reduce.1 = bf16[16,2,512]{2,1,0:T(2,128)(2,1)S(1)} all-reduce(f32[16,2,512]{2,1,0:T(2,128)S(1)} %copy.41), channel_id=4, replica_groups=mesh['kpt'=4,'pw'=8] {'kpt'}, use_global_device_ids=true, to_apply=%region_11.0.clone | all-reduce | flops 16384 | bytes 98304
  197.9 28.9 %reduce-scatter.12.cloned.1.call-done = f32[64,8]{1,0:T(8,128)} async-done(((f32[512,8]{1,0:T(8,128)}), f32[64,8]{1,0:T(8,128)}) %reduce-scatter.12.cloned.1.call-update) | async-done | bytes 2064
  227.9 14.0 %all-reduce.4 = (f32[2]{0:T(128)S(1)}, f32[2]{0:T(128)S(1)}, f32[2]{0:T(128)S(1)}) all-reduce(f32[2]{0:T(128)S(1)} %get-tuple-element.21, f32[2]{0:T(128)S(1)} %get-tuple-element.20, f32[2]{0:T(128)S(1)} %get-tuple-element.19), channel_id=1, replica_groups=mesh['kpt'=4,'pw'=8] {'pw'}, use_global_device_ids=true, to_apply=%region_20.0 | all-reduce | flops 6 | bytes 48 | tf_op jit(solution)/shard_map/psum | solution.py:57
  241.9 8.0 %all-reduce.7 = (f32[2]{0:T(128)S(1)}, f32[2]{0:T(128)S(1)}, f32[2]{0:T(128)S(1)}) all-reduce(f32[2]{0:T(128)S(1)} %get-tuple-element.28, f32[2]{0:T(128)S(1)} %get-tuple-element.29, f32[2]{0:T(128)S(1)} %get-tuple-element.30), channel_id=1, replica_groups=mesh['kpt'=4,'pw'=8] {'kpt'}, use_global_device_ids=true, to_apply=%region_21.0 | all-reduce | flops 6 | bytes 48 | tf_op jit(solution)/shard_map/psum | solution.py:56
  250.1 14.6 %all_gather.33 = bf16[2,4,512]{1,0,2:T(2,128)(2,1)S(1)} all-gather(bf16[2,4,64]{1,0,2:T(2,128)(2,1)S(1)} %copy.43), channel_id=1, replica_groups=mesh['kpt'=4,'pw'=8] {'pw'}, dimensions={2}, use_global_device_ids=true | all-gather | bytes 9216 | tf_op jit(solution)/shard_map/all_gather | solution.py:35
  265.3 9.0 %all_gather.34 = bf16[16,2,512]{2,1,0:T(2,128)(2,1)S(1)} all-gather(bf16[4,2,512]{2,1,0:T(2,128)(2,1)S(1)} %convolution_convert_fusion), channel_id=1, replica_groups=mesh['kpt'=4,'pw'=8] {'kpt'}, dimensions={0}, use_global_device_ids=true | all-gather | bytes 40960 | tf_op jit(solution)/shard_map/all_gather | solution.py:11
  274.3 14.2 %all_gather.35 = bf16[16,2,4096]{2,0,1:T(8,128)(2,1)S(1)} all-gather(bf16[16,2,512]{2,0,1:T(8,128)(2,1)S(1)} %copy.45), channel_id=1, replica_groups=mesh['kpt'=4,'pw'=8] {'pw'}, dimensions={2}, use_global_device_ids=true | all-gather | bytes 294912 | tf_op jit(solution)/shard_map/all_gather | solution.py:15
  288.6 10.8 %fusion.12 = f32[4,16,2,512]{3,1,0,2:T(8,128)S(1)} fusion(bf16[4,512,4096]{2,1,0:T(8,128)(2,1)} %param.14, bf16[16,2,4096]{2,0,1:T(8,128)(2,1)S(1)} %all_gather.35), kind=kOutput, calls=%fused_computation.8 | convolution fusion | flops 536870912 | bytes 17301504 | tf_op jit(solution)/shard_map/qsg,kvg->qkvs/dot_general | solution.py:12
  299.8 15.0 %all-reduce.2 = bf16[16,2,512]{2,1,0:T(2,128)(2,1)S(1)} all-reduce(f32[16,2,512]{2,1,0:T(2,128)S(1)} %copy.46), channel_id=6, replica_groups=mesh['kpt'=4,'pw'=8] {'kpt'}, use_global_device_ids=true, to_apply=%region_22.0.clone | all-reduce | flops 16384 | bytes 98304
  318.6 28.9 %reduce-scatter.14.cloned.1.call-done = f32[64,8]{1,0:T(8,128)} async-done(((f32[512,8]{1,0:T(8,128)}), f32[64,8]{1,0:T(8,128)}) %reduce-scatter.14.cloned.1.call-update) | async-done | bytes 2064
  348.7 14.0 %all-reduce.3 = (f32[2]{0:T(128)S(1)}, f32[2]{0:T(128)S(1)}, f32[2]{0:T(128)S(1)}) all-reduce(f32[2]{0:T(128)S(1)} %get-tuple-element.18, f32[2]{0:T(128)S(1)} %get-tuple-element.17, f32[2]{0:T(128)S(1)} %get-tuple-element.16), channel_id=1, replica_groups=mesh['kpt'=4,'pw'=8] {'pw'}, use_global_device_ids=true, to_apply=%region_31.0 | all-reduce | flops 6 | bytes 48 | tf_op jit(solution)/shard_map/psum | solution.py:57
  362.7 8.0 %all-reduce.6 = (f32[2]{0:T(128)S(1)}, f32[2]{0:T(128)S(1)}, f32[2]{0:T(128)S(1)}) all-reduce(f32[2]{0:T(128)S(1)} %get-tuple-element.25, f32[2]{0:T(128)S(1)} %get-tuple-element.26, f32[2]{0:T(128)S(1)} %get-tuple-element.27), channel_id=1, replica_groups=mesh['kpt'=4,'pw'=8] {'kpt'}, use_global_device_ids=true, to_apply=%region_32.0 | all-reduce | flops 6 | bytes 48 | tf_op jit(solution)/shard_map/psum | solution.py:56
  (71 shorter events, 22.0 us)
Async XLA Ops:
  7.2 15.6 %copy-start = (bf16[4,512,512]{2,1,0:T(8,128)(2,1)S(1)}, bf16[4,512,512]{2,1,0:T(8,128)(2,1)}, u32[]{:S(2)}) copy-start(bf16[4,512,512]{2,1,0:T(8,128)(2,1)} %param.13) | copy-start | bytes 6291460
  7.2 98.5 %reduce-scatter.10.cloned.1.call-start = ((), (), s32[]{:S(2)}) async-start(), calls=%async_computation.3 | async-start | bytes 294912
  45.6 10.8 %copy-start.1 = (s32[16,16]{1,0:T(8,128)S(1)}, s32[16,16]{1,0:T(8,128)}, u32[]{:S(2)}) copy-start(s32[16,16]{1,0:T(8,128)} %param.15) | copy-start | bytes 3076
  45.6 26.3 %copy-start.7 = (u32[32]{0:T(128)S(1)}, u32[32]{0:T(128)}, u32[]{:S(2)}) copy-start(u32[32]{0:T(128)} %constant.29) | copy-start | bytes 388
  73.2 33.4 %copy-start.2 = (f32[2,4,64]{2,1,0:T(4,128)S(1)}, f32[2,4,64]{2,1,0:T(4,128)}, u32[]{:S(2)}) copy-start(f32[2,4,64]{2,1,0:T(4,128)} %param.9) | copy-start | bytes 6148
  73.2 33.4 %copy-start.4 = (f32[4,64]{1,0:T(4,128)S(1)}, f32[4,64]{1,0:T(4,128)}, u32[]{:S(2)}) copy-start(f32[4,64]{1,0:T(4,128)} %param.8) | copy-start | bytes 3076
  73.2 33.4 %copy-start.5 = (f32[2,4,64]{2,1,0:T(4,128)S(1)}, f32[2,4,64]{2,1,0:T(4,128)}, u32[]{:S(2)}) copy-start(f32[2,4,64]{2,1,0:T(4,128)} %param.10) | copy-start | bytes 6148
  73.2 33.4 %copy-start.6 = (f32[2]{0:T(128)S(1)}, f32[2]{0:T(128)}, u32[]{:S(2)}) copy-start(f32[2]{0:T(128)} %param.11) | copy-start | bytes 28
  77.1 149.6 %reduce-scatter.12.cloned.1.call-start = ((), (), s32[]{:S(2)}) async-start(), calls=%async_computation.4 | async-start | bytes 294912
  197.8 149.8 %reduce-scatter.14.cloned.1.call-start = ((), (), s32[]{:S(2)}) async-start(), calls=%async_computation.5 | async-start | bytes 294912
  250.0 122.1 %copy-start.3 = (f32[2,4,64]{2,1,0:T(4,128)}, f32[2,4,64]{2,1,0:T(4,128)S(1)}, u32[]{:S(2)}) copy-start(f32[2,4,64]{2,1,0:T(4,128)S(1)} %get-tuple-element.45) | copy-start | bytes 6148
Sparse Core Ops, SparseCore 0:
  77.2 28.3 reduce-scatter.9
  197.9 28.7 reduce-scatter.11
  318.8 28.7 reduce-scatter.13
